TPU v7x, 32 devices: a whole 2x2x4 slice. The times are simulated.
32 devices in a mesh: row: 8 (over z, x), col: 4 (over y, core).
Axes of the slice: x: 2, y: 2, z: 4, core: 2. Of those that a mesh axis runs over, the one named last changes fastest.
Arguments:
- amplitudes: float32 [200, 10, 10, 1024], P('row', None, None, 'col'), may hold values from -6 to 6
- old_blocks: int32 [8, 25], replicated, may hold values from 0 to 135, as said below
- old_counts: int32 [8], replicated, may hold values from 1 to 25, as said below
- new_phase: int32 [1], replicated, may hold values from 0 to 7
- fock: float32 [160, 160], P('row'), may hold values from -0.5 to 0.5
Outputs:
- contracted: float32 [16, 10, 160, 1024], P('row', None, None, 'col')
Inputs may be any that keep to these rules, and one draw needn't show every extreme that they name: `old_blocks`: over the live slots of all row devices every tile pair id 0 to 135 stands exactly once; ids in slots that are not live are arbitrary. For every residue r mod 8, at most 8 live blocks of one row device hold a tile whose index is r mod 8, and some device reaches 8 for some r. `old_counts`: the counts sum to 136; some device has exactly 25.
All inputs are finite; a program needn't handle non-finite values.
Results may differ from a plain program's by a relative error of at most 0.00007.
Values sent between devices are 32-bit elements; how exact they have to be, the bound alone decides.
No kernel may reach another device: no remote copies, remote signals or barrier semaphores. Data moves between devices by JAX's collectives and lax.ppermute only.
A program may use at most 128 MiB of HBM per device.

v0:
```python
import jax
import jax.numpy as jnp
import numpy as np
from jax import lax
from jax.sharding import PartitionSpec as P

NT = 16


def pair_table():
    table = np.zeros((NT, NT), np.int32)
    first_tile = np.zeros((NT * (NT + 1) // 2,), np.int32)
    second_tile = np.zeros((NT * (NT + 1) // 2,), np.int32)
    for first in range(NT):
        for second in range(NT):
            low = min(first, second)
            high = max(first, second)
            ident = low * NT - low * (low - 1) // 2 + (high - low)
            table[first, second] = ident
            first_tile[ident] = low
            second_tile[ident] = high
    return (table, first_tile, second_tile)


def body(amplitudes, old_blocks, old_counts, new_phase, fock):
    nrows = lax.axis_size("row")
    myself = lax.axis_index("row")
    slots = amplitudes.shape[0]
    tile = amplitudes.shape[1]
    occ_dev = amplitudes.shape[3]
    width = fock.shape[1]
    per_dev = NT // nrows
    nblocks = NT * (NT + 1) // 2
    phase = new_phase[0]
    table, first_tile, second_tile = pair_table()
    live = jnp.arange(slots, dtype=jnp.int32)[None, :] < old_counts[:, None]
    flat = amplitudes.reshape(slots, tile * tile * occ_dev)
    fock_full = lax.all_gather(fock, "row", axis=0, tiled=True)
    match_ids = old_blocks.reshape(-1)
    match_live = live.reshape(-1)
    my_ids = lax.dynamic_slice_in_dim(old_blocks, myself, 1, 0)[0]
    my_live = lax.dynamic_slice_in_dim(live, myself, 1, 0)[0]
    owner_low = (jnp.asarray(first_tile)[my_ids] + phase) % nrows
    owner_high = (jnp.asarray(second_tile)[my_ids] + phase) % nrows
    target = jnp.arange(nrows, dtype=jnp.int32)[:, None]
    sending = ((owner_low[None, :] == target) | (owner_high[None, :] == target)) & my_live[None, :]
    capacity = per_dev * ((slots - 2) // 8 + 2)
    ordinal = jnp.cumsum(sending.astype(jnp.int32), axis=1) - 1
    packing = (
        ordinal[:, None, :] == jnp.arange(capacity, dtype=jnp.int32)[None, :, None]
    ) & sending[:, None, :]
    payload = jnp.einsum(
        "dcs,sp->dcp", packing.astype(jnp.float32), flat, precision=lax.Precision.HIGHEST
    )
    filled = jnp.any(packing, axis=2)
    sent_ids = jnp.sum(jnp.where(packing, my_ids[None, None, :], 0), axis=2)
    sent_ids = jnp.where(filled, sent_ids, nblocks)
    payload_in, ids_in = (
        lax.all_to_all(payload, "row", split_axis=0, concat_axis=0, tiled=True),
        lax.all_to_all(sent_ids, "row", split_axis=0, concat_axis=0, tiled=True),
    )
    received = payload_in
    match_ids = ids_in.reshape(-1)
    match_live = match_ids < nblocks
    received = received.reshape(-1, tile * tile * occ_dev)
    index = jnp.arange(tile, dtype=jnp.int32)
    results = []
    for within in range(per_dev):
        column_tile = (myself - phase) % nrows + within * nrows
        needed = jnp.asarray(table)[:, column_tile]
        picker = ((match_ids[None, :] == needed[:, None]) & match_live[None, :]).astype(jnp.float32)
        chosen = jnp.dot(picker, received, precision=lax.Precision.HIGHEST)
        chosen = chosen.reshape(NT, tile, tile, occ_dev)
        c_global = jnp.arange(NT, dtype=jnp.int32)[:, None, None] * tile + index[None, :, None]
        b_global = column_tile * tile + index[None, None, :]
        below = (c_global < b_global)[:, :, :, None]
        above = (c_global > b_global)[:, :, :, None]
        dense = jnp.where(below, chosen, jnp.where(above, -jnp.swapaxes(chosen, 1, 2), 0.0))
        dense = dense.reshape(width, tile, occ_dev)
        outcome = jnp.einsum("ac,cbj->baj", fock_full, dense, precision=lax.Precision.HIGHEST)
        results.append(outcome)
    return jnp.stack(results, 0)


def solution(mesh):
    return jax.shard_map(
        body,
        mesh=mesh,
        in_specs=(P("row", None, None, "col"), P(), P(), P(), P("row", None)),
        out_specs=P("row", None, None, "col"),
        check_vma=False,
    )
```

profile of v0, /device:TPU:0, one launch (start us, length us, event | category | flops | bytes accessed | tf_op | source)
XLA Modules:
  0.0 239.0 jit_solution(3944722288822886608)
XLA Ops:
  0.0 0.7 fusion.30
  0.7 0.7 fusion.31
  1.4 1.4 gather_fusion
  2.8 1.4 gather_fusion.1
  4.8 0.7 iota_compare_fusion.1
  6.2 0.6 broadcast_select_fusion
  6.8 7.3 %all-to-all-start = ((s32[8,1,8]{2,1,0:T(1,128)}), s32[8,1,8]{2,1,0:T(1,128)S(1)}, u32[]{:S(2)}, u32[]{:S(2)}) async-start(s32[8,1,8]{2,1,0:T(1,128)} %bitcast.6), calls=%async_computation | async-start | bytes 8192 | tf_op jit(solution)/shard_map/all_to_all | solution.py:60
  14.1 5.4 %copy.19 = f32[25,10,10,256]{3,2,1,0:T(8,128)} copy(f32[25,10,10,256]{3,0,2,1:T(8,128)} %param.8) | data formatting | bytes 5120000 | tf_op args[0]
  19.5 3.2 %reshape.256 = f32[25,25600,1]{1,0,2:T(8,128)S(1)} reshape(f32[25,10,10,256]{3,2,1,0:T(8,128)} %copy.19) | data formatting | bytes 5120000 | tf_op jit(solution)/shard_map/reshape | solution.py:37
  22.7 4.6 %fusion.7 = f32[8,8,25600]{2,1,0:T(8,128)} fusion(f32[25,25600,1]{1,0,2:T(8,128)S(1)} %reshape.256, s32[8,25]{1,0:T(8,128)S(1)} %broadcast_add_fusion, pred[8,25]{1,0:T(8,128)(4,1)S(1)} %get-tuple-element.6), kind=kOutput, calls=%fused_computation.22 | convolution fusion | flops 491523200 | bytes 9114600 | tf_op jit(solution)/shard_map/dcs,sp->dcp/dot_general | solution.py:52
  27.4 6.1 %all-to-all-start.1 = ((f32[8,8,25600]{2,1,0:T(8,128)}), f32[8,8,25600]{2,1,0:T(8,128)}, u32[]{:S(2)}, u32[]{:S(2)}) async-start(f32[8,8,25600]{2,1,0:T(8,128)} %fusion.7), calls=%async_computation.1 | async-start | bytes 13107200 | tf_op jit(solution)/shard_map/all_to_all | solution.py:59
  33.5 163.5 %all-gather = f32[8,20,160]{2,1,0:T(8,128)S(1)} all-gather(f32[1,20,160]{2,1,0:T(8,128)S(1)} %bitcast.59), channel_id=1, replica_groups=mesh['row'=8,'col'=4] {'row'}, dimensions={0}, use_global_device_ids=true | all-gather | bytes 115200 | tf_op jit(solution)/shard_map/all_gather | solution.py:38
  197.0 0.7 fusion.26
  198.4 0.7 reduce.3
  199.1 8.8 %dot_general.21 = f32[10,10,256,64]{2,1,0,3:T(8,128)} reshape(f32[25600,64]{0,1:T(8,128)} %bitcast.11) | data formatting | bytes 13107200 | tf_op jit(solution)/shard_map/dot_general | solution.py:72
  208.0 9.2 %fusion.2 = f32[16,10,10,256]{3,0,2,1:T(8,128)S(1)} fusion(f32[10,10,256,64]{2,1,0,3:T(8,128)} %dot_general.21, s32[64]{0:T(128)S(1)} %eq.100, s32[16]{0:T(128)S(1)} %get-tuple-element.13, pred[64]{0:T(512)(128)(4,1)S(1)} %broadcast_compare_fusion.4), kind=kOutput, calls=%fused_computation.4 | convolution fusion | flops 314574848 | bytes 8192384 | tf_op jit(solution)/shard_map/dot_general | solution.py:72
  217.8 1.1 copy.22
  218.8 1.3 reshape.236
  220.1 9.2 %fusion = f32[16,10,10,256]{3,0,2,1:T(8,128)S(1)} fusion(f32[10,10,256,64]{2,1,0,3:T(8,128)} %dot_general.21, s32[64]{0:T(128)S(1)} %eq.100, s32[16]{0:T(128)S(1)} %get-tuple-element.14, pred[64]{0:T(512)(128)(4,1)S(1)} %broadcast_compare_fusion.4), kind=kOutput, calls=%fused_computation.2 | convolution fusion | flops 314574848 | bytes 8192384 | tf_op jit(solution)/shard_map/dot_general | solution.py:72
  229.9 1.1 copy.25
  231.0 1.3 reshape.237
  232.3 3.2 %convolution_bitcast_fusion.1 = f32[1,10,160,256]{3,2,1,0:T(8,128)S(1)} fusion(f32[160,10,256]{2,0,1:T(8,128)} %reshape.236, f32[160,160,1]{1,0,2:T(8,128)S(1)} %reshape.258), kind=kOutput, calls=%fused_computation.14 | convolution fusion | flops 786432000 | bytes 3379200 | tf_op jit(solution)/shard_map/ac,cbj->baj/dot_general | solution.py:80
  235.4 1.6 convolution_bitcast_fusion
  237.0 1.9 pad_maximum_fusion
  (24 shorter events, 2.6 us)
Async XLA Ops:
  6.8 20.5 %all-to-all-start = ((s32[8,1,8]{2,1,0:T(1,128)}), s32[8,1,8]{2,1,0:T(1,128)S(1)}, u32[]{:S(2)}, u32[]{:S(2)}) async-start(s32[8,1,8]{2,1,0:T(1,128)} %bitcast.6), calls=%async_computation | async-start | bytes 8192 | tf_op jit(solution)/shard_map/all_to_all | solution.py:60
  27.3 6.1 %copy-start.1 = (f32[20,160]{1,0:T(8,128)S(1)}, f32[20,160]{1,0:T(8,128)}, u32[]{:S(2)}) copy-start(f32[20,160]{1,0:T(8,128)} %param.12) | copy-start | bytes 38404
  27.4 171.8 %all-to-all-start.1 = ((f32[8,8,25600]{2,1,0:T(8,128)}), f32[8,8,25600]{2,1,0:T(8,128)}, u32[]{:S(2)}, u32[]{:S(2)}) async-start(f32[8,8,25600]{2,1,0:T(8,128)} %fusion.7), calls=%async_computation.1 | async-start | bytes 13107200 | tf_op jit(solution)/shard_map/all_to_all | solution.py:59
  232.3 3.2 %copy-start = (f32[160,10,256]{2,0,1:T(8,128)S(1)}, f32[160,10,256]{2,0,1:T(8,128)}, u32[]{:S(2)}) copy-start(f32[160,10,256]{2,0,1:T(8,128)} %reshape.237) | copy-start | bytes 4915204
where the time goes:
time: 240 us; the launch traced here: 239 us
  blocking collectives  163 us (68%)
  matrix products  27.7 us (12%)
  local copies, waits for them, and re-layouts  27 us (11%)
  starting transfers between devices  13.4 us (6%)
  other arithmetic  6.61 us (3%)
    all_gather x1, blocking collectives, body(): fock_full = lax.all_gather(fock, 'row', axis=0, tiled=True)  163 us
    dot_general x2, matrix products, body(): chosen = jnp.dot(picker, received, precision=lax.Precision.HIGHEST)  18.3 us
    dot_general x1, local copies, waits for them, and re-layouts, body(): chosen = jnp.dot(picker, received, precision=lax.Precision.HIGHEST)  8.85 us
    all_to_all x1, starting transfers between devices, body(): lax.all_to_all(sent_ids, 'row', split_axis=0, concat_axis=0, tiled=True)  7.28 us
    all_to_all x1, starting transfers between devices, body(): lax.all_to_all(payload, 'row', split_axis=0, concat_axis=0, tiled=True)  6.13 us
    unnamed x6, local copies, waits for them, and re-layouts  5.44 us
  transfers between devices with their start and end apart: 2, of which 0 were waited for; matrix products, arithmetic and copies ran while one was open for 6% of the time, Pallas kernels for 0%

commit v1 on v0

--- a/solution.py
+++ b/solution.py
@@ -35,7 +35,14 @@
     table, first_tile, second_tile = pair_table()
     live = jnp.arange(slots, dtype=jnp.int32)[None, :] < old_counts[:, None]
     flat = amplitudes.reshape(slots, tile * tile * occ_dev)
-    fock_full = lax.all_gather(fock, "row", axis=0, tiled=True)
+    ways, here = (lax.axis_size("row"), lax.axis_index("row"))
+    fock_full, reach = (fock, 1)
+    while reach < ways:
+        theirs = lax.ppermute(fock_full, "row", [(d, d ^ reach) for d in range(ways)])
+        mine_first = jnp.concatenate([fock_full, theirs], axis=0)
+        theirs_first = jnp.concatenate([theirs, fock_full], axis=0)
+        fock_full = jnp.where(here & reach == 0, mine_first, theirs_first)
+        reach = 2 * reach
     match_ids = old_blocks.reshape(-1)
     match_live = live.reshape(-1)
     my_ids = lax.dynamic_slice_in_dim(old_blocks, myself, 1, 0)[0]

time: 240 us -> 222 us (0.925)
  blocking collectives: 163 us -> 0 us
  waiting for transfers between devices: 0.01 us -> 136 us
  starting transfers between devices: 13.4 us -> 21 us
    all_gather x1 -> x0, blocking collectives: 163 us -> none  [body(): fock_full = lax.all_gather(fock, 'row', axis=0, tiled=True)]
    ppermute x0 -> x3, waiting for transfers between devices: none -> 101 us  [body(): lax.ppermute(fock_full, 'row', [(d, d ^ reach) for d in range(ways)])]
    all_to_all x1, waiting for transfers between devices: 0.01 us -> 35.3 us  [body(): lax.all_to_all(payload, 'row', split_axis=0, concat_axis=0, tiled=True)]
    ppermute x0 -> x3, starting transfers between devices: none -> 7.56 us  [body(): lax.ppermute(fock_full, 'row', [(d, d ^ reach) for d in range(ways)])]
    unnamed x6 -> x5, local copies, waits for them, and re-layouts: 5.44 us -> 5.42 us
  transfers between devices with their start and end apart: 2 -> 5, of which waited for: 0 -> 3; matrix products, arithmetic and copies ran while one was open for 6% -> 23% of each run, Pallas kernels for 0% -> 0%
where the time goes in v1:
time: 222 us
  waiting for transfers between devices  136 us (61%)
  local copies, waits for them, and re-layouts  28.4 us (13%)
  matrix products  27.7 us (12%)
  starting transfers between devices  21 us (9%)
  other arithmetic  7.51 us (3%)
    ppermute x3, waiting for transfers between devices, body(): lax.ppermute(fock_full, 'row', [(d, d ^ reach) for d in range(ways)])  101 us
    all_to_all x1, waiting for transfers between devices, body(): lax.all_to_all(payload, 'row', split_axis=0, concat_axis=0, tiled=True)  35.3 us
    dot_general x2, matrix products, body(): chosen = jnp.dot(picker, received, precision=lax.Precision.HIGHEST)  18.3 us
    dot_general x1, local copies, waits for them, and re-layouts, body(): chosen = jnp.dot(picker, received, precision=lax.Precision.HIGHEST)  8.82 us
    ppermute x3, starting transfers between devices, body(): lax.ppermute(fock_full, 'row', [(d, d ^ reach) for d in range(ways)])  7.56 us
    all_to_all x1, starting transfers between devices, body(): lax.all_to_all(sent_ids, 'row', split_axis=0, concat_axis=0, tiled=True)  7.28 us
    all_to_all x1, starting transfers between devices, body(): lax.all_to_all(payload, 'row', split_axis=0, concat_axis=0, tiled=True)  6.13 us
    unnamed x5, local copies, waits for them, and re-layouts  5.42 us
  transfers between devices with their start and end apart: 5, of which 3 were waited for; matrix products, arithmetic and copies ran while one was open for 23% of the time, Pallas kernels for 0%

profile of v1, /device:TPU:0, one launch (start us, length us, event | category | flops | bytes accessed | tf_op | source)
XLA Modules:
  0.0 221.5 jit_solution(14902357993389569415)
XLA Ops:
  1.4 1.4 gather_fusion
  2.8 1.4 gather_fusion.1
  6.8 7.3 %all-to-all-start = ((s32[8,1,8]{2,1,0:T(1,128)}), s32[8,1,8]{2,1,0:T(1,128)S(1)}, u32[]{:S(2)}, u32[]{:S(2)}) async-start(s32[8,1,8]{2,1,0:T(1,128)} %bitcast.6), calls=%async_computation | async-start | bytes 8192 | tf_op jit(solution)/shard_map/all_to_all | solution.py:67
  14.1 5.4 %copy.19 = f32[25,10,10,256]{3,2,1,0:T(8,128)} copy(f32[25,10,10,256]{3,0,2,1:T(8,128)} %param.8) | data formatting | bytes 5120000 | tf_op args[0]
  19.5 3.2 %reshape.254 = f32[25,25600,1]{1,0,2:T(8,128)S(1)} reshape(f32[25,10,10,256]{3,2,1,0:T(8,128)} %copy.19) | data formatting | bytes 5120000 | tf_op jit(solution)/shard_map/reshape | solution.py:37
  22.7 4.6 %fusion.12 = f32[8,8,25600]{2,1,0:T(8,128)} fusion(f32[25,25600,1]{1,0,2:T(8,128)S(1)} %reshape.254, s32[8,25]{1,0:T(8,128)S(1)} %broadcast_add_fusion, pred[8,25]{1,0:T(8,128)(4,1)S(1)} %get-tuple-element.6), kind=kOutput, calls=%fused_computation.28 | convolution fusion | flops 491523200 | bytes 9114600 | tf_op jit(solution)/shard_map/dcs,sp->dcp/dot_general | solution.py:59
  27.4 6.1 %all-to-all-start.1 = ((f32[8,8,25600]{2,1,0:T(8,128)}), f32[8,8,25600]{2,1,0:T(8,128)}, u32[]{:S(2)}, u32[]{:S(2)}) async-start(f32[8,8,25600]{2,1,0:T(8,128)} %fusion.12), calls=%async_computation.1 | async-start | bytes 13107200 | tf_op jit(solution)/shard_map/all_to_all | solution.py:66
  33.5 2.0 collective-permute-start
  37.6 48.8 %collective-permute-done = f32[20,160]{1,0:T(8,128)S(1)} collective-permute-done((f32[20,160]{1,0:T(8,128)S(1)}, f32[20,160]{1,0:T(8,128)S(1)}, u32[]{:S(2)}, u32[]{:S(2)}) %collective-permute-start) | collective-permute-done | bytes 12832 | tf_op jit(solution)/shard_map/ppermute | solution.py:41
  86.5 1.6 collective-permute-start.1
  88.1 52.0 %collective-permute-done.1 = f32[40,160]{1,0:T(8,128)S(1)} collective-permute-done((f32[40,160]{1,0:T(8,128)S(1)}, f32[40,160]{1,0:T(8,128)S(1)}, u32[]{:S(2)}, u32[]{:S(2)}) %collective-permute-start.1) | collective-permute-done | bytes 25632 | tf_op jit(solution)/shard_map/ppermute | solution.py:41
  140.2 3.9 %collective-permute-start.2 = (f32[80,160]{1,0:T(8,128)S(1)}, f32[80,160]{1,0:T(8,128)S(1)}, u32[]{:S(2)}, u32[]{:S(2)}) collective-permute-start(f32[80,160]{1,0:T(8,128)S(1)} %maximum_select_fusion.1), channel_id=1, source_target_pairs={{0,16},{4,20},{8,24},{12,28},{16,0},{20,4},{24,8},{28,12},{1,17},{... | collective-permute-start | bytes 153608 | tf_op jit(solution)/shard_map/ppermute | solution.py:41
  144.1 35.3 %all-to-all-done.1 = f32[8,8,25600]{2,1,0:T(8,128)} async-done(((f32[8,8,25600]{2,1,0:T(8,128)}), f32[8,8,25600]{2,1,0:T(8,128)}, u32[]{:S(2)}, u32[]{:S(2)}) %all-to-all-start.1) | async-done | bytes 6553632 | tf_op jit(solution)/shard_map/all_to_all | solution.py:66
  179.4 8.8 %dot_general.21 = f32[10,10,256,64]{2,1,0,3:T(8,128)} reshape(f32[25600,64]{0,1:T(8,128)} %bitcast.11) | data formatting | bytes 13107200 | tf_op jit(solution)/shard_map/dot_general | solution.py:79
  188.2 9.2 %fusion.2 = f32[16,10,10,256]{3,0,2,1:T(8,128)S(1)} fusion(f32[10,10,256,64]{2,1,0,3:T(8,128)} %dot_general.21, s32[64]{0:T(128)S(1)} %eq.109, s32[16]{0:T(128)S(1)} %get-tuple-element.13, pred[64]{0:T(512)(128)(4,1)S(1)} %broadcast_compare_fusion.4), kind=kOutput, calls=%fused_computation.4 | convolution fusion | flops 314574848 | bytes 8192384 | tf_op jit(solution)/shard_map/dot_general | solution.py:79
  197.4 9.2 %fusion = f32[16,10,10,256]{3,0,2,1:T(8,128)S(1)} fusion(f32[10,10,256,64]{2,1,0,3:T(8,128)} %dot_general.21, s32[64]{0:T(128)S(1)} %eq.109, s32[16]{0:T(128)S(1)} %get-tuple-element.14, pred[64]{0:T(512)(128)(4,1)S(1)} %broadcast_compare_fusion.4), kind=kOutput, calls=%fused_computation.2 | convolution fusion | flops 314574848 | bytes 8192384 | tf_op jit(solution)/shard_map/dot_general | solution.py:79
  207.2 1.5 fusion.4
  208.7 1.1 copy.22
  209.7 1.3 reshape.236
  211.0 2.5 %copy.25 = f32[16,10,10,256]{3,1,0,2:T(8,128)S(1)} copy(f32[16,10,10,256]{3,0,2,1:T(8,128)} %fusion.4) | data formatting | bytes 3276800 | tf_op jit(solution)/shard_map/jit(_where)/select_n | solution.py:85
  213.5 1.3 reshape.237
  214.8 3.2 %convolution_bitcast_fusion.1 = f32[1,10,160,256]{3,2,1,0:T(8,128)S(1)} fusion(f32[160,10,256]{2,0,1:T(8,128)} %reshape.236, f32[80,160]{1,0:T(8,128)S(1)} %collective-permute-done.2, f32[80,160]{1,0:T(8,128)S(1)} %maximum_select_fusion.1, pred[]{:T(512)S(6)} %eq.114), kind=kOutput, calls=%fused_computation.14 | convolution fusion | flops 786508800 | bytes 3379201 | tf_op jit(solution)/shard_map/ac,cbj->baj/dot_general | solution.py:87
  218.0 1.6 convolution_bitcast_fusion
  219.6 1.9 pad_maximum_fusion
  (30 shorter events, 6.1 us)
Async XLA Ops:
  6.8 20.5 %all-to-all-start = ((s32[8,1,8]{2,1,0:T(1,128)}), s32[8,1,8]{2,1,0:T(1,128)S(1)}, u32[]{:S(2)}, u32[]{:S(2)}) async-start(s32[8,1,8]{2,1,0:T(1,128)} %bitcast.6), calls=%async_computation | async-start | bytes 8192 | tf_op jit(solution)/shard_map/all_to_all | solution.py:67
  27.4 6.1 %copy-start.1 = (f32[20,160]{1,0:T(8,128)S(1)}, f32[20,160]{1,0:T(8,128)}, u32[]{:S(2)}) copy-start(f32[20,160]{1,0:T(8,128)} %param.12) | copy-start | bytes 38404
  27.4 152.0 %all-to-all-start.1 = ((f32[8,8,25600]{2,1,0:T(8,128)}), f32[8,8,25600]{2,1,0:T(8,128)}, u32[]{:S(2)}, u32[]{:S(2)}) async-start(f32[8,8,25600]{2,1,0:T(8,128)} %fusion.12), calls=%async_computation.1 | async-start | bytes 13107200 | tf_op jit(solution)/shard_map/all_to_all | solution.py:66
  33.5 53.0 %collective-permute-start = (f32[20,160]{1,0:T(8,128)S(1)}, f32[20,160]{1,0:T(8,128)S(1)}, u32[]{:S(2)}, u32[]{:S(2)}) collective-permute-start(f32[20,160]{1,0:T(8,128)S(1)} %copy-done.1), channel_id=1, source_target_pairs={{0,4},{4,0},{8,12},{12,8},{16,20},{20,16},{24,28},{28,24},{1,5},{5... | collective-permute-start | bytes 38408 | tf_op jit(solution)/shard_map/ppermute | solution.py:41
  86.5 53.7 %collective-permute-start.1 = (f32[40,160]{1,0:T(8,128)S(1)}, f32[40,160]{1,0:T(8,128)S(1)}, u32[]{:S(2)}, u32[]{:S(2)}) collective-permute-start(f32[40,160]{1,0:T(8,128)S(1)} %maximum_select_fusion.2), channel_id=1, source_target_pairs={{0,8},{4,12},{8,0},{12,4},{16,24},{20,28},{24,16},{28,20},{1,9},{5... | collective-permute-start | bytes 76808 | tf_op jit(solution)/shard_map/ppermute | solution.py:41
  140.2 74.6 %collective-permute-start.2 = (f32[80,160]{1,0:T(8,128)S(1)}, f32[80,160]{1,0:T(8,128)S(1)}, u32[]{:S(2)}, u32[]{:S(2)}) collective-permute-start(f32[80,160]{1,0:T(8,128)S(1)} %maximum_select_fusion.1), channel_id=1, source_target_pairs={{0,16},{4,20},{8,24},{12,28},{16,0},{20,4},{24,8},{28,12},{1,17},{... | collective-permute-start | bytes 153608 | tf_op jit(solution)/shard_map/ppermute | solution.py:41
  214.8 3.2 %copy-start = (f32[160,10,256]{2,0,1:T(8,128)S(1)}, f32[160,10,256]{2,0,1:T(8,128)}, u32[]{:S(2)}) copy-start(f32[160,10,256]{2,0,1:T(8,128)} %reshape.237) | copy-start | bytes 4915204
